TPU v7x, 512 devices: a whole 4x4x16 slice. The times are simulated.
512 devices in a mesh: bytes: 16 (over z), ctx: 8 (over x, core), tp: 4 (over y).
Axes of the slice: x: 4, y: 4, z: 16, core: 2. Of those that a mesh axis runs over, the one named last changes fastest.
Arguments:
- byte_values_sequence: int32 [24576], P(('bytes', 'ctx')), may hold values from 0 to 255
- offsets: int32 [24576], P(('bytes', 'ctx')), may hold values from 0 to 168, as said below
- byte_table: bfloat16 [256, 1024], replicated, may hold values from -6 to 6
- byte_query: bfloat16 [1024, 1024], P(None, 'tp'), may hold values from -1 to 1
- byte_key: bfloat16 [1024, 1024], P(None, 'tp'), may hold values from -16 to 16
- byte_value: bfloat16 [1024, 1024], P(None, 'tp'), may hold values from -0.1875 to 0.1875
- latent_query: bfloat16 [1024, 4096], P(None, ('ctx', 'tp')), may hold values from -1 to 1
- latent_key: bfloat16 [1024, 4096], P(None, ('ctx', 'tp')), may hold values from -16 to 16
- latent_value: bfloat16 [1024, 4096], P(None, ('ctx', 'tp')), may hold values from -0.1875 to 0.1875
- decode_weight: bfloat16 [4096, 1024], P(('ctx', 'tp')), may hold values from -1 to 1
Outputs:
- byte_output: bfloat16 [24576, 1024], P(('bytes', 'ctx'), 'tp')
Inputs may be any that keep to these rules, and one draw needn't show every extreme that they name: offsets[i] is 0 where a patch starts and offsets[i - 1] + 1 elsewhere; the first byte of every device's 192 bytes starts a patch; one device's bytes hold 24 to 72 patch starts and the bytes of the devices of one index of bytes hold at most 384; both most values are reached in every draw.
All inputs are finite; a program needn't handle non-finite values.
Results may differ from a plain program's by a relative error of at most 0.017.
Values may be sent and summed in bfloat16 or wider, within the bound.
No kernel may reach another device: no remote copies, remote signals or barrier semaphores. Data moves between devices by JAX's collectives and lax.ppermute only.
A program may use at most 64 MiB of HBM per device.

v0:
```python
import math
import jax
import jax.numpy as jnp
from jax import lax
from jax.sharding import PartitionSpec as P

DB = 1024
HEADS_B = 16
HEAD_L = 128
EPSILON = 1e-06
NEGATIVE = -1e30
FARAWAY = 1 << 30


def from_behind(value, axis, steps):
    count = lax.axis_size(axis)
    first, last = (max(0, -steps), min(count, count - steps))
    return lax.ppermute(value, axis, [(source, source + steps) for source in range(first, last)])


def copy_for_each(array, axis):
    copies = jnp.broadcast_to(array, (lax.axis_size(axis), *array.shape))
    return lax.all_to_all(copies, axis, split_axis=0, concat_axis=0, tiled=True)


def joined_along(tiles, dim):
    tiles = jnp.moveaxis(tiles, 0, dim)
    lengths = tiles.shape
    return tiles.reshape(*lengths[:dim], lengths[dim] * lengths[dim + 1], *lengths[dim + 2 :])


def collect(array, axis, dim):
    tiles = copy_for_each(array, axis)
    return joined_along(tiles, dim)


def sent_together(arrays, axis, dim, along):
    widths = [a.shape[along] for a in arrays]
    both = jnp.concatenate(arrays, axis=along)
    filled = lax.all_gather(both, axis, axis=dim, tiled=True)
    return tuple(jnp.split(filled, [sum(widths[:k]) for k in range(1, len(widths))], axis=along))


def cut_along(array, dim, count):
    before, after = (array.shape[:dim], array.shape[dim + 1 :])
    return jnp.moveaxis(array.reshape(*before, count, -1, *after), dim, 0)


def sent_and_summed(array, axis, dim):
    tiles = cut_along(array, dim, lax.axis_size(axis))
    arrived = lax.all_to_all(tiles, axis, split_axis=0, concat_axis=0, tiled=True)
    return arrived.astype(jnp.float32).sum(axis=0)


def norm_rows(values):
    values = values.astype(jnp.float32)
    return values * lax.rsqrt(jnp.mean(values * values, axis=-1, keepdims=True) + EPSILON)


def project(inputs, weight):
    return jnp.dot(inputs, weight, preferred_element_type=jnp.float32).astype(jnp.bfloat16)


def byte_project(byte_values_sequence, byte_table, weights):
    onehot = (
        byte_values_sequence[:, None] == jnp.arange(byte_table.shape[0], dtype=jnp.int32)[None, :]
    ).astype(jnp.bfloat16)
    embedded = jnp.dot(onehot, byte_table, preferred_element_type=jnp.float32)
    normed = norm_rows(embedded).astype(jnp.bfloat16)
    return tuple((project(normed, weight) for weight in weights))


def per_device(
    byte_values_sequence,
    offsets,
    byte_table,
    byte_query,
    byte_key,
    byte_value,
    latent_query,
    latent_key,
    latent_value,
    decode_weight,
):
    row_count = byte_values_sequence.shape[0]
    channels = byte_query.shape[1]
    heads_here = HEADS_B * channels // DB
    head_feature_width = channels // heads_here
    ctx_count = lax.axis_size("ctx")
    tp_count = lax.axis_size("tp")
    slot_cap = 3 * row_count // 8
    block_index = lax.axis_index(("bytes", "ctx"))
    byte_window_queries, byte_window_keys, values_b = byte_project(
        byte_values_sequence, byte_table, (byte_query, byte_key, byte_value)
    )
    earlier_ids = from_behind(byte_values_sequence, ("bytes", "ctx"), 1)
    keys_e, values_e = byte_project(earlier_ids, byte_table, (byte_key, byte_value))
    keys_w = jnp.concatenate([keys_e, byte_window_keys], axis=0).reshape(
        2 * row_count, heads_here, head_feature_width
    )
    values_w = jnp.concatenate([values_e, values_b], axis=0).reshape(
        2 * row_count, heads_here, head_feature_width
    )
    queries_w = byte_window_queries.reshape(row_count, heads_here, head_feature_width)
    query_pos = jnp.arange(row_count, dtype=jnp.int32)[:, None]
    key_pos = jnp.arange(2 * row_count, dtype=jnp.int32)[None, :]
    allowed_b = (
        (key_pos > query_pos)
        & (key_pos <= query_pos + row_count)
        & ((key_pos >= row_count) | (block_index > 0))
    )
    scores_b = jnp.einsum(
        "qhd,khd->hqk", queries_w, keys_w, preferred_element_type=jnp.float32
    ) / math.sqrt(head_feature_width)
    scores_b = jnp.where(allowed_b[None], scores_b, NEGATIVE)
    highest_b = jnp.max(scores_b, axis=-1, keepdims=True)
    weights_b = jnp.where(allowed_b[None], jnp.exp(scores_b - highest_b), 0.0)
    totals_b = jnp.sum(weights_b, axis=-1)
    blended = jnp.einsum(
        "hqk,khd->qhd", weights_b.astype(jnp.bfloat16), values_w, preferred_element_type=jnp.float32
    )
    encoded = (blended / totals_b.T[:, :, None]).reshape(row_count, channels).astype(jnp.bfloat16)
    starts = (offsets == 0).astype(jnp.int32)
    local_patch = jnp.cumsum(starts) - 1
    members = local_patch[None, :] == jnp.arange(slot_cap, dtype=jnp.int32)[:, None]
    patch_sums = jnp.dot(members.astype(jnp.bfloat16), encoded, preferred_element_type=jnp.float32)
    lengths = jnp.sum(members.astype(jnp.float32), axis=1)
    pooled = (patch_sums / jnp.maximum(lengths, 1.0)[:, None]).astype(jnp.bfloat16)
    gathered, patch_counts = (
        collect(pooled, ("ctx", "tp"), 0),
        collect(local_patch[-1:] + 1, ("ctx", "tp"), 0),
    )
    features = gathered.reshape(ctx_count, tp_count, slot_cap, channels).transpose(0, 2, 1, 3)
    features = features.reshape(ctx_count * slot_cap, tp_count * channels)
    patch_counts = patch_counts.reshape(ctx_count, tp_count)[:, 0]
    slot_ids = jnp.arange(slot_cap, dtype=jnp.int32)
    block_ids = lax.axis_index("bytes") * ctx_count + jnp.arange(ctx_count, dtype=jnp.int32)
    positions = jnp.where(
        slot_ids[None, :] < patch_counts[:, None],
        block_ids[:, None] * slot_cap + slot_ids[None, :],
        FARAWAY,
    ).reshape(-1)
    capacity = ctx_count * row_count // 4
    running = jnp.cumsum((positions < FARAWAY).astype(jnp.int32))
    targets = jnp.arange(capacity, dtype=jnp.int32)
    chosen = jnp.minimum(jnp.searchsorted(running, targets + 1), running.shape[0] - 1)
    features = features[chosen]
    positions = jnp.where(targets < running[-1], positions[chosen], FARAWAY)
    latent_in = norm_rows(features).astype(jnp.bfloat16)
    queries_l = project(latent_in, latent_query)
    keys_l = project(latent_in, latent_key)
    values_l = project(latent_in, latent_value)
    query_rows = queries_l.shape[0]
    heads_latent = queries_l.shape[1] // HEAD_L
    queries_h = queries_l.reshape(query_rows, heads_latent, HEAD_L)
    initial = (
        jnp.full((heads_latent, query_rows), NEGATIVE, jnp.float32),
        jnp.zeros((heads_latent, query_rows), jnp.float32),
        jnp.zeros((query_rows, heads_latent, HEAD_L), jnp.float32),
    )
    running_state = initial
    keys_p, values_p, places_p = (
        *sent_together((keys_l, values_l), "bytes", 0, 1),
        lax.all_gather(positions, "bytes", axis=0, tiled=True),
    )
    span_rows = keys_p.shape[0]

    def attend_block(state, step_index):
        highest, totals, accumulated = state
        keys_s = lax.dynamic_slice_in_dim(keys_p, step_index * query_rows, query_rows, 0).reshape(
            query_rows, heads_latent, HEAD_L
        )
        values_s = lax.dynamic_slice_in_dim(
            values_p, step_index * query_rows, query_rows, 0
        ).reshape(query_rows, heads_latent, HEAD_L)
        places = lax.dynamic_slice_in_dim(places_p, step_index * query_rows, query_rows, 0)
        attention_scores = jnp.einsum(
            "qhd,khd->hqk", queries_h, keys_s, preferred_element_type=jnp.float32
        ) / math.sqrt(HEAD_L)
        allowed = (places[None, :] <= positions[:, None])[None]
        highest_new = jnp.maximum(
            highest, jnp.max(jnp.where(allowed, attention_scores, NEGATIVE), axis=-1)
        )
        factor = jnp.exp(highest - highest_new)
        weights = jnp.where(allowed, jnp.exp(attention_scores - highest_new[:, :, None]), 0.0)
        totals = totals * factor + jnp.sum(weights, axis=-1)
        mixed_in = jnp.einsum(
            "hqk,khd->qhd",
            weights.astype(jnp.bfloat16),
            values_s,
            preferred_element_type=jnp.float32,
        )
        accumulated = accumulated * factor.T[:, :, None] + mixed_in
        return ((highest_new, totals, accumulated), None)

    running_state, _ = lax.scan(
        attend_block, running_state, jnp.arange(span_rows // query_rows, dtype=jnp.int32)
    )
    highest_l, totals_l, accumulated_l = running_state
    latent_out = (
        (accumulated_l / totals_l.T[:, :, None])
        .reshape(query_rows, heads_latent * HEAD_L)
        .astype(jnp.bfloat16)
    )
    shares = sent_and_summed(
        jnp.dot(latent_out, decode_weight, preferred_element_type=jnp.float32).astype(jnp.bfloat16),
        ("ctx", "tp"),
        0,
    )
    summed = collect(shares.astype(jnp.bfloat16), ("ctx", "tp"), 0).astype(shares.dtype)
    before = jnp.sum(
        jnp.where(jnp.arange(ctx_count, dtype=jnp.int32) < lax.axis_index("ctx"), patch_counts, 0)
    )
    mine = lax.dynamic_slice_in_dim(summed, lax.axis_index("tp") * channels, channels, 1)
    decoded_bytes = mine[before + local_patch]
    return (encoded.astype(jnp.float32) + decoded_bytes).astype(jnp.bfloat16)


def solution(mesh):
    return jax.shard_map(
        per_device,
        mesh=mesh,
        in_specs=(
            P(("bytes", "ctx")),
            P(("bytes", "ctx")),
            P(),
            P(None, "tp"),
            P(None, "tp"),
            P(None, "tp"),
            P(None, ("ctx", "tp")),
            P(None, ("ctx", "tp")),
            P(None, ("ctx", "tp")),
            P(("ctx", "tp"), None),
        ),
        out_specs=P(("bytes", "ctx"), "tp"),
        check_vma=False,
    )
```

profile of v0, /device:TPU:1, one launch (start us, length us, event | category | flops | bytes accessed | tf_op | source)
XLA Modules:
  0.0 257.1 jit_solution(15806933889242681807)
XLA Ops:
  6.5 4.6 %collective-permute-start = (s32[192]{0:T(256)}, s32[192]{0:T(256)S(1)}, u32[]{:S(2)}, u32[]{:S(2)}) collective-permute-start(s32[192]{0:T(256)} %param.14), channel_id=1, source_target_pairs={{0,4},{4,8},{8,12},{12,16},{16,20},{20,24},{24,28},{28,32},{32,36}... | collective-permute-start | bytes 2312 | tf_op jit(solution)/shard_map/ppermute | solution.py:18
  14.9 7.3 %all-to-all-start = ((s32[32,1,1]{2,1,0:T(1,128)}), s32[32,1,1]{2,1,0:T(1,128)S(1)}, u32[]{:S(2)}, u32[]{:S(2)}) async-start(s32[32,1,1]{2,1,0:T(1,128)} %broadcast_in_dim.111), calls=%async_computation | async-start | bytes 32768 | tf_op jit(solution)/shard_map/all_to_all | solution.py:23
  22.3 1.1 multiply_reduce_fusion
  24.8 0.9 convolution_convert_fusion.7
  26.6 2.6 %all-to-all-done = s32[32,1,1]{2,1,0:T(1,128)S(1)} async-done(((s32[32,1,1]{2,1,0:T(1,128)}), s32[32,1,1]{2,1,0:T(1,128)S(1)}, u32[]{:S(2)}, u32[]{:S(2)}) %all-to-all-start) | async-done | bytes 160 | tf_op jit(solution)/shard_map/all_to_all | solution.py:23
  32.2 0.7 fusion.53
  33.0 1.3 fusion.25
  36.1 1.1 broadcast_in_dim.118
  37.2 4.8 %all-to-all-start.1 = ((bf16[32,72,256]{2,1,0:T(8,128)(2,1)}), bf16[32,72,256]{2,1,0:T(8,128)(2,1)S(1)}, u32[]{:S(2)}, u32[]{:S(2)}) async-start(bf16[32,72,256]{2,1,0:T(8,128)(2,1)} %broadcast_in_dim.118), calls=%async_computation.1 | async-start | bytes 2359296 | tf_op jit(solution)/shard_map/all_to_all | solution.py:23
  42.0 19.8 %while.39 = (s32[]{:T(128)}, u32[384]{0:T(512)S(1)}, u32[384]{0:T(512)S(1)}, s32[576]{0:T(1024)S(1)}, s32[]{:T(128)}, /*index=5*/s32[]{:T(128)}, s32[]{}) while((s32[]{:T(128)}, u32[384]{0:T(512)S(1)}, u32[384]{0:T(512)S(1)}, s32[576]{0:T(1024)S(1)}, s32[]{:T(128)}, /*index=5*/s32[]{:T(128)}, s32[]{}) %tuple.72), condition=%wide.region_10.11_spmd.clone, body=%wide.region_9.10_spmd.clone.sunk | while | flops 8324 | bytes 29541 | solution.py:146
  42.1 1.9 gather_fusion
  44.1 1.9 gather_fusion
  46.0 1.9 gather_fusion
  48.0 1.9 gather_fusion
  50.0 1.9 gather_fusion
  52.0 1.9 gather_fusion
  54.0 1.9 gather_fusion
  56.0 1.9 gather_fusion
  57.9 1.9 gather_fusion
  59.9 1.9 gather_fusion
  62.7 2.1 gather_fusion.2
  66.2 0.7 pad_maximum_fusion.2
  66.9 1.9 gather_fusion.1
  70.1 29.0 %all-gather = s32[16,1,384]{2,1,0:T(1,128)S(1)} all-gather(s32[1,1,384]{2,1,0:T(1,128)S(1)} %reshape.249), channel_id=1, replica_groups=mesh['bytes'=16,'ctx'=8,'tp'=4] {'bytes'}, dimensions={0}, use_global_device_ids=true | all-gather | bytes 26112 | tf_op jit(solution)/shard_map/all_gather | solution.py:164
  99.5 38.2 %all-gather.3.cloned.1.call-done = bf16[6144,256]{0,1:T(8,128)(2,1)} async-done(((bf16[384,256]{0,1:T(8,128)(2,1)}), bf16[6144,256]{0,1:T(8,128)(2,1)}) %all-gather.3.cloned.1.call-update) | async-done | bytes 3145744 | tf_op jit(solution)/shard_map/all_gather | solution.py:40
  137.7 3.3 %fusion.52 = (bf16[6144,128]{0,1:T(8,128)(2,1)S(1)}, bf16[6144,128]{0,1:T(8,128)(2,1)}) fusion(bf16[6144,256]{0,1:T(8,128)(2,1)} %all-gather.3.cloned.1.call-done), kind=kLoop, calls=%fused_computation.120 | loop fusion | bytes 6291456 | tf_op jit(solution)/shard_map/split | solution.py:41
  141.0 51.5 %while.40 = (s32[]{:T(128)}, f32[1,384]{1,0:T(1,128)S(1)}, f32[1,384]{1,0:T(1,128)S(1)}, f32[384,1,128]{0,2,1:T(8,128)S(1)}, s32[16]{0:T(128)S(1)}, /*index=5*/s...) while((s32[]{:T(128)}, f32[1,384]{1,0:T(1,128)S(1)}, ...), condition=%wide.region_15.16_spmd.clone, body=%wide.region_12.15_spmd.clone.sunk | while | flops 77416712 | bytes 2498263 | solution.py:196
  142.4 1.2 fusion.84
  145.7 1.2 fusion.84
  148.9 1.2 fusion.84
  152.1 1.2 fusion.84
  155.3 1.2 fusion.84
  158.5 1.2 fusion.84
  161.8 1.2 fusion.84
  165.0 1.2 fusion.84
  168.2 1.2 fusion.84
  171.4 1.2 fusion.84
  174.6 1.2 fusion.84
  177.8 1.2 fusion.84
  181.1 1.2 fusion.84
  184.3 1.2 fusion.84
  187.5 1.2 fusion.84
  190.7 1.2 fusion.84
  193.1 33.0 %all_to_all.21 = bf16[32,12,1024]{2,1,0:T(8,128)(2,1)S(1)} all-to-all(bf16[32,12,1024]{2,1,0:T(8,128)(2,1)S(1)} %reshape.208), channel_id=1, replica_groups=mesh['bytes'=16,'ctx'=8,'tp'=4] {'ctx','tp'}, dimensions={0} | all-to-all | bytes 1572864 | tf_op jit(solution)/shard_map/all_to_all | solution.py:51
  226.3 1.1 broadcast_in_dim.119
  227.4 4.8 %all-to-all-start.3 = ((bf16[32,12,1024]{2,1,0:T(8,128)(2,1)}), bf16[32,12,1024]{2,1,0:T(8,128)(2,1)S(1)}, u32[]{:S(2)}, u32[]{:S(2)}) async-start(bf16[32,12,1024]{2,1,0:T(8,128)(2,1)} %broadcast_in_dim.119), calls=%async_computation.3 | async-start | bytes 2097152 | tf_op jit(solution)/shard_map/all_to_all | solution.py:23
  233.6 14.9 %all-to-all-done.3 = bf16[32,12,1024]{2,1,0:T(8,128)(2,1)S(1)} async-done(((bf16[32,12,1024]{2,1,0:T(8,128)(2,1)}), bf16[32,12,1024]{2,1,0:T(8,128)(2,1)S(1)}, u32[]{:S(2)}, u32[]{:S(2)}) %all-to-all-start.3) | async-done | bytes 786464 | tf_op jit(solution)/shard_map/all_to_all | solution.py:23
  248.7 0.9 gather_fusion.3
  (284 shorter events, 37.9 us)
Async XLA Ops:
  6.5 15.8 %copy-start = (bf16[256,1024]{1,0:T(8,128)(2,1)S(1)}, bf16[256,1024]{1,0:T(8,128)(2,1)}, u32[]{:S(2)}) copy-start(bf16[256,1024]{1,0:T(8,128)(2,1)} %param.16) | copy-start | bytes 1572868
  6.5 24.7 %collective-permute-start = (s32[192]{0:T(256)}, s32[192]{0:T(256)S(1)}, u32[]{:S(2)}, u32[]{:S(2)}) collective-permute-start(s32[192]{0:T(256)} %param.14), channel_id=1, source_target_pairs={{0,4},{4,8},{8,12},{12,16},{16,20},{20,24},{24,28},{28,32},{32,36}... | collective-permute-start | bytes 2312 | tf_op jit(solution)/shard_map/ppermute | solution.py:18
  12.5 0.6 copy-start.13
  13.1 10.4 %copy-start.17 = (s32[192]{0:T(256)}, s32[192]{0:T(256)S(1)}, u32[]{:S(2)}) copy-start(s32[192]{0:T(256)S(1)} %slice_add_fusion) | copy-start | bytes 2308
  14.9 14.2 %all-to-all-start = ((s32[32,1,1]{2,1,0:T(1,128)}), s32[32,1,1]{2,1,0:T(1,128)S(1)}, u32[]{:S(2)}, u32[]{:S(2)}) async-start(s32[32,1,1]{2,1,0:T(1,128)} %broadcast_in_dim.111), calls=%async_computation | async-start | bytes 32768 | tf_op jit(solution)/shard_map/all_to_all | solution.py:23
  22.3 1.3 copy-start.1
  23.5 1.0 copy-start.4
  23.7 1.1 copy-start.2
  26.4 5.8 %copy-start.6 = (pred[192,384]{1,0:T(8,128)(4,1)}, pred[192,384]{1,0:T(8,128)(4,1)S(1)}, u32[]{:S(2)}) copy-start(pred[192,384]{1,0:T(8,128)(4,1)S(1)} %fusion.34) | copy-start | bytes 221188
  26.6 5.7 %copy-start.3 = (bf16[192,256]{0,1:T(8,128)(2,1)}, bf16[192,256]{0,1:T(8,128)(2,1)S(1)}, u32[]{:S(2)}) copy-start(bf16[192,256]{0,1:T(8,128)(2,1)S(1)} %copy.33) | copy-start | bytes 294916
  30.0 0.6 copy-start.15
  31.7 0.6 copy-start.11
  33.0 1.4 copy-start.12
  33.0 1.7 copy-start.5
  34.4 0.9 copy-start.7
  35.2 0.6 copy-start.18
  35.2 0.6 copy-start.22
  35.8 1.4 copy-start.9
  37.2 24.7 %all-to-all-start.1 = ((bf16[32,72,256]{2,1,0:T(8,128)(2,1)}), bf16[32,72,256]{2,1,0:T(8,128)(2,1)S(1)}, u32[]{:S(2)}, u32[]{:S(2)}) async-start(bf16[32,72,256]{2,1,0:T(8,128)(2,1)} %broadcast_in_dim.118), calls=%async_computation.1 | async-start | bytes 2359296 | tf_op jit(solution)/shard_map/all_to_all | solution.py:23
  42.0 95.8 %all-gather.3.cloned.1.call-start = ((), (), s32[]{:S(2)}) async-start(), calls=%async_computation.4 | async-start | bytes 3342336 | tf_op jit(solution)/shard_map/all_gather | solution.py:40
  62.7 2.3 copy-start.19
  64.7 1.0 copy-start.20
  66.9 32.2 %copy-start.21 = (bf16[1024,128]{1,0:T(8,128)(2,1)S(1)}, bf16[1024,128]{1,0:T(8,128)(2,1)}, u32[]{:S(2)}) copy-start(bf16[1024,128]{1,0:T(8,128)(2,1)} %param.20) | copy-start | bytes 786436
  141.0 51.5 %copy-start.8 = (bf16[128,1024]{1,0:T(8,128)(2,1)S(1)}, bf16[128,1024]{1,0:T(8,128)(2,1)}, u32[]{:S(2)}) copy-start(bf16[128,1024]{1,0:T(8,128)(2,1)} %param.23) | copy-start | bytes 786436
  227.4 4.8 %copy-start.16 = (s32[8]{0:T(128)S(1)}, s32[8]{0:T(128)}, u32[]{:S(2)}) copy-start(s32[8]{0:T(128)} %copy-done.15) | copy-start | bytes 100
  227.4 5.4 %copy-start.14 = (s32[256]{0:T(256)S(1)}, s32[256]{0:T(256)}, u32[]{:S(2)}) copy-start(s32[256]{0:T(256)} %copy-done.13) | copy-start | bytes 3076
  227.4 6.1 %copy-start.10 = (bf16[192,4,64]{0,2,1:T(8,128)(2,1)S(1)}, bf16[192,4,64]{0,2,1:T(8,128)(2,1)}, u32[]{:S(2)}) copy-start(bf16[192,4,64]{0,2,1:T(8,128)(2,1)} %copy-done.9) | copy-start | bytes 294916
  227.4 21.1 %all-to-all-start.3 = ((bf16[32,12,1024]{2,1,0:T(8,128)(2,1)}), bf16[32,12,1024]{2,1,0:T(8,128)(2,1)S(1)}, u32[]{:S(2)}, u32[]{:S(2)}) async-start(bf16[32,12,1024]{2,1,0:T(8,128)(2,1)} %broadcast_in_dim.119), calls=%async_computation.3 | async-start | bytes 2097152 | tf_op jit(solution)/shard_map/all_to_all | solution.py:23
Sparse Core Ops, SparseCore 0:
  67.0 70.6 all-gather.2
where the time goes:
time: 258 us; the launch traced here: 257 us
  blocking collectives  62 us (24%)
  waiting for transfers between devices  55.7 us (22%)
  local copies, waits for them, and re-layouts  47.7 us (18%)
  matrix products  32.5 us (13%)
  starting transfers between devices  21.5 us (8%)
  between operations  14.6 us (6%)
  loops' own time  12.5 us (5%)
  other arithmetic  10.6 us (4%)
    all_gather x1, waiting for transfers between devices, sent_together(): filled = lax.all_gather(both, axis, axis=dim, tiled=True)  38.2 us
    all_to_all x1, blocking collectives, sent_and_summed(): lax.all_to_all(tiles, axis, split_axis=0, concat_axis=0, tiled=True)  33 us
    all_gather x1, blocking collectives, per_device(): lax.all_gather(positions, 'bytes', axis=0, tiled=True)  29 us
    dot_general x16, matrix products, attend_block(): jnp.einsum('qhd,khd->hqk', queries_h, keys_s, preferred_element_type=jnp....  18.9 us
    gather x10, local copies, waits for them, and re-layouts, per_device(): jnp.searchsorted(running, targets + 1)  18.9 us
    all_to_all x3, waiting for transfers between devices, copy_for_each(): return lax.all_to_all(copies, axis, split_axis=0, concat_axis=0, tiled=True)  17.5 us
    all_to_all x3, starting transfers between devices, copy_for_each(): return lax.all_to_all(copies, axis, split_axis=0, concat_axis=0, tiled=True)  16.9 us
    another operation x1, loops' own time, per_device(): lax.scan(attend_block, running_state, jnp.arange(span_rows // query_rows,...  11.9 us
  transfers between devices with their start and end apart: 5, of which 3 were waited for; matrix products, arithmetic and copies ran while one was open for 12% of the time, Pallas kernels for 0%

commit v1 on v0

--- a/solution.py
+++ b/solution.py
@@ -1,8 +1,10 @@
+import functools
 import math
 import jax
 import jax.numpy as jnp
 from jax import lax
 from jax.sharding import PartitionSpec as P
+from jax.lax import axis_index, axis_size, ppermute
 
 DB = 1024
 HEADS_B = 16
@@ -10,6 +12,39 @@
 EPSILON = 1e-06
 NEGATIVE = -1e30
 FARAWAY = 1 << 30
+
+
+def manage_strips_all(page, at_axis):
+    page = jnp.moveaxis(page, 0, at_axis)
+    frame_out = page.shape
+    q_next = page.reshape(
+        *frame_out[:at_axis], frame_out[at_axis] * frame_out[at_axis + 1], *frame_out[at_axis + 2 :]
+    )
+    return q_next
+
+
+def _report_teams(raw, comm_axis, d0):
+    n_slots = axis_size(comm_axis)
+    column = [(to_i, (to_i + 1) % n_slots) for to_i in range(n_slots)]
+    leaves = [(c, rr) for rr, c in column]
+    current_value, x_now = ([], [])
+    pp = 0
+    while pp < n_slots - 1:
+        if pp % 2 == 0:
+            current_value.append(
+                ppermute(current_value[-1] if current_value else raw, comm_axis, column)
+            )
+        else:
+            x_now.append(ppermute(x_now[-1] if x_now else raw, comm_axis, leaves))
+        pp = pp + 1
+    fresh = jnp.stack([*current_value[::-1], raw, *x_now])
+    v_next = axis_index(comm_axis) - len(current_value)
+    fresh = fresh[(jnp.arange(n_slots) - v_next) % n_slots]
+    latest = manage_strips_all(fresh, d0)
+    return latest
+
+
+_extend_tiles = functools.partial(_report_teams, comm_axis="bytes", d0=0)
 
 
 def from_behind(value, axis, steps):
@@ -161,7 +196,7 @@
     running_state = initial
     keys_p, values_p, places_p = (
         *sent_together((keys_l, values_l), "bytes", 0, 1),
-        lax.all_gather(positions, "bytes", axis=0, tiled=True),
+        _extend_tiles(positions),
     )
     span_rows = keys_p.shape[0]
 

time: 258 us -> 255 us (0.988)
  starting transfers between devices: 21.5 us -> 74.4 us
  blocking collectives: 62 us -> 32.9 us
  waiting for transfers between devices: 55.7 us -> 30.7 us
    ppermute x0 -> x15, starting transfers between devices: none -> 53.6 us  [the longest x7 36.6 us: _report_teams(): x_now.append(ppermute(x_now[-1] if x_now else raw, comm_axis, leaves))]
    all_gather x1, waiting for transfers between devices: 38.2 us -> 9.2 us  [sent_together(): filled = lax.all_gather(both, axis, axis=dim, tiled=True)]
    all_gather x1 -> x0, blocking collectives: 29 us -> none  [per_device(): lax.all_gather(positions, 'bytes', axis=0, tiled=True)]
    ppermute x0 -> x15, waiting for transfers between devices: none -> 2.84 us  [the longest x8 2.82 us: _report_teams(): ppermute(current_value[-1] if current_value else raw, comm_axis, column)]
  transfers between devices with their start and end apart: 5 -> 20, of which waited for: 3 -> 4; matrix products, arithmetic and copies ran while one was open for 12% -> 13% of each run, Pallas kernels for 0% -> 0%
where the time goes in v1:
time: 255 us; the launch traced here: 254 us
  starting transfers between devices  74.4 us (29%)
  local copies, waits for them, and re-layouts  46.9 us (18%)
  blocking collectives  32.9 us (13%)
  matrix products  31 us (12%)
  waiting for transfers between devices  30.7 us (12%)
  between operations  14.9 us (6%)
  loops' own time  12.4 us (5%)
  other arithmetic  10.7 us (4%)
    ppermute x7, starting transfers between devices, _report_teams(): x_now.append(ppermute(x_now[-1] if x_now else raw, comm_axis, leaves))  36.6 us
    all_to_all x1, blocking collectives, sent_and_summed(): lax.all_to_all(tiles, axis, split_axis=0, concat_axis=0, tiled=True)  32.9 us
    dot_general x16, matrix products, attend_block(): jnp.einsum('qhd,khd->hqk', queries_h, keys_s, preferred_element_type=jnp....  19 us
    gather x10, local copies, waits for them, and re-layouts, per_device(): jnp.searchsorted(running, targets + 1)  18.9 us
    all_to_all x3, waiting for transfers between devices, copy_for_each(): return lax.all_to_all(copies, axis, split_axis=0, concat_axis=0, tiled=True)  18.6 us
    ppermute x8, starting transfers between devices, _report_teams(): ppermute(current_value[-1] if current_value else raw, comm_axis, column)  17 us
    all_to_all x3, starting transfers between devices, copy_for_each(): return lax.all_to_all(copies, axis, split_axis=0, concat_axis=0, tiled=True)  16.2 us
    another operation x1, loops' own time, per_device(): lax.scan(attend_block, running_state, jnp.arange(span_rows // query_rows,...  11.9 us
  transfers between devices with their start and end apart: 20, of which 4 were waited for; matrix products, arithmetic and copies ran while one was open for 13% of the time, Pallas kernels for 0%

profile of v1, /device:TPU:1, one launch (start us, length us, event | category | flops | bytes accessed | tf_op | source)
XLA Modules:
  0.0 253.9 jit_solution(942530859513558394)
XLA Ops:
  6.5 4.6 %collective-permute-start = (s32[192]{0:T(256)}, s32[192]{0:T(256)S(1)}, u32[]{:S(2)}, u32[]{:S(2)}) collective-permute-start(s32[192]{0:T(256)} %param.14), channel_id=1, source_target_pairs={{0,4},{4,8},{8,12},{12,16},{16,20},{20,24},{24,28},{28,32},{32,36}... | collective-permute-start | bytes 2312 | tf_op jit(solution)/shard_map/ppermute | solution.py:53
  14.3 7.3 %all-to-all-start = ((s32[32,1,1]{2,1,0:T(1,128)}), s32[32,1,1]{2,1,0:T(1,128)S(1)}, u32[]{:S(2)}, u32[]{:S(2)}) async-start(s32[32,1,1]{2,1,0:T(1,128)} %broadcast_in_dim.114), calls=%async_computation | async-start | bytes 32768 | tf_op jit(solution)/shard_map/all_to_all | solution.py:58
  24.8 3.7 %all-to-all-done = s32[32,1,1]{2,1,0:T(1,128)S(1)} async-done(((s32[32,1,1]{2,1,0:T(1,128)}), s32[32,1,1]{2,1,0:T(1,128)S(1)}, u32[]{:S(2)}, u32[]{:S(2)}) %all-to-all-start) | async-done | bytes 160 | tf_op jit(solution)/shard_map/all_to_all | solution.py:58
  34.5 4.3 %all-to-all-start.1 = ((bf16[32,72,256]{2,1,0:T(8,128)(2,1)}), bf16[32,72,256]{2,1,0:T(8,128)(2,1)S(1)}, u32[]{:S(2)}, u32[]{:S(2)}) async-start(bf16[32,72,256]{2,1,0:T(8,128)(2,1)} %broadcast_in_dim.122), calls=%async_computation.1 | async-start | bytes 2359296 | tf_op jit(solution)/shard_map/all_to_all | solution.py:58
  38.8 19.8 %while.39 = (s32[]{:T(128)}, u32[384]{0:T(512)S(1)}, u32[384]{0:T(512)S(1)}, s32[576]{0:T(1024)S(1)}, s32[]{:T(128)}, /*index=5*/s32[]{:T(128)}, s32[]{}) while((s32[]{:T(128)}, u32[384]{0:T(512)S(1)}, u32[384]{0:T(512)S(1)}, s32[576]{0:T(1024)S(1)}, s32[]{:T(128)}, /*index=5*/s32[]{:T(128)}, s32[]{}) %tuple.72), condition=%wide.region_10.11_spmd.clone, body=%wide.region_9.10_spmd.clone.sunk | while | flops 8324 | bytes 29541 | solution.py:181
  38.9 1.9 gather_fusion
  40.9 1.9 gather_fusion
  42.8 1.9 gather_fusion
  44.8 1.9 gather_fusion
  46.8 1.9 gather_fusion
  48.8 1.9 gather_fusion
  50.8 1.9 gather_fusion
  52.7 1.9 gather_fusion
  54.7 1.9 gather_fusion
  56.7 1.9 gather_fusion
  59.5 2.1 gather_fusion.3
  64.3 1.9 gather_fusion.1
  66.9 3.5 %collective-permute-start.1 = (s32[384]{0:T(512)S(1)}, s32[384]{0:T(512)S(1)}, u32[]{:S(2)}, u32[]{:S(2)}) collective-permute-start(s32[384]{0:T(512)S(1)} %fusion.42), channel_id=1, source_target_pairs={{0,32},{32,64},{64,96},{96,128},{128,160},{160,192},{192,224},{224... | collective-permute-start | bytes 4616 | tf_op jit(solution)/shard_map/ppermute | solution.py:35
  70.4 9.1 %collective-permute-start.9 = (s32[384]{0:T(512)S(1)}, s32[384]{0:T(512)S(1)}, u32[]{:S(2)}, u32[]{:S(2)}) collective-permute-start(s32[384]{0:T(512)S(1)} %fusion.42), channel_id=1, source_target_pairs={{32,0},{64,32},{96,64},{128,96},{160,128},{192,160},{224,192},{256... | collective-permute-start | bytes 4616 | tf_op jit(solution)/shard_map/ppermute | solution.py:38
  79.6 1.9 collective-permute-start.2
  81.5 4.6 %collective-permute-start.10 = (s32[384]{0:T(512)S(1)}, s32[384]{0:T(512)S(1)}, u32[]{:S(2)}, u32[]{:S(2)}) collective-permute-start(s32[384]{0:T(512)S(1)} %collective-permute-done.9), channel_id=1, source_target_pairs={{32,0},{64,32},{96,64},{128,96},{160,128},{192,160},{224,192},{256... | collective-permute-start | bytes 4616 | tf_op jit(solution)/shard_map/ppermute | solution.py:38
  86.1 1.9 collective-permute-start.3
  88.0 4.6 %collective-permute-start.11 = (s32[384]{0:T(512)S(1)}, s32[384]{0:T(512)S(1)}, u32[]{:S(2)}, u32[]{:S(2)}) collective-permute-start(s32[384]{0:T(512)S(1)} %collective-permute-done.10), channel_id=1, source_target_pairs={{32,0},{64,32},{96,64},{128,96},{160,128},{192,160},{224,192},{256... | collective-permute-start | bytes 4616 | tf_op jit(solution)/shard_map/ppermute | solution.py:38
  92.6 1.9 collective-permute-start.4
  94.6 4.6 %collective-permute-start.12 = (s32[384]{0:T(512)S(1)}, s32[384]{0:T(512)S(1)}, u32[]{:S(2)}, u32[]{:S(2)}) collective-permute-start(s32[384]{0:T(512)S(1)} %collective-permute-done.11), channel_id=1, source_target_pairs={{32,0},{64,32},{96,64},{128,96},{160,128},{192,160},{224,192},{256... | collective-permute-start | bytes 4616 | tf_op jit(solution)/shard_map/ppermute | solution.py:38
  99.2 1.9 collective-permute-start.5
  101.1 4.6 %collective-permute-start.13 = (s32[384]{0:T(512)S(1)}, s32[384]{0:T(512)S(1)}, u32[]{:S(2)}, u32[]{:S(2)}) collective-permute-start(s32[384]{0:T(512)S(1)} %collective-permute-done.12), channel_id=1, source_target_pairs={{32,0},{64,32},{96,64},{128,96},{160,128},{192,160},{224,192},{256... | collective-permute-start | bytes 4616 | tf_op jit(solution)/shard_map/ppermute | solution.py:38
  105.7 1.9 collective-permute-start.6
  107.7 4.6 %collective-permute-start.14 = (s32[384]{0:T(512)S(1)}, s32[384]{0:T(512)S(1)}, u32[]{:S(2)}, u32[]{:S(2)}) collective-permute-start(s32[384]{0:T(512)S(1)} %collective-permute-done.13), channel_id=1, source_target_pairs={{32,0},{64,32},{96,64},{128,96},{160,128},{192,160},{224,192},{256... | collective-permute-start | bytes 4616 | tf_op jit(solution)/shard_map/ppermute | solution.py:38
  112.2 1.9 collective-permute-start.7
  114.2 4.6 %collective-permute-start.15 = (s32[384]{0:T(512)S(1)}, s32[384]{0:T(512)S(1)}, u32[]{:S(2)}, u32[]{:S(2)}) collective-permute-start(s32[384]{0:T(512)S(1)} %collective-permute-done.14), channel_id=1, source_target_pairs={{32,0},{64,32},{96,64},{128,96},{160,128},{192,160},{224,192},{256... | collective-permute-start | bytes 4616 | tf_op jit(solution)/shard_map/ppermute | solution.py:38
  118.8 1.9 collective-permute-start.8
  121.6 2.8 %collective-permute-done.8 = s32[384]{0:T(512)S(1)} collective-permute-done((s32[384]{0:T(512)S(1)}, s32[384]{0:T(512)S(1)}, u32[]{:S(2)}, u32[]{:S(2)}) %collective-permute-start.8) | collective-permute-done | bytes 1568 | tf_op jit(solution)/shard_map/ppermute | solution.py:35
  125.4 9.2 %all-gather.2.cloned.1.call-done = bf16[6144,256]{0,1:T(8,128)(2,1)} async-done(((bf16[384,256]{0,1:T(8,128)(2,1)}), bf16[6144,256]{0,1:T(8,128)(2,1)}) %all-gather.2.cloned.1.call-update) | async-done | bytes 3145744 | tf_op jit(solution)/shard_map/all_gather | solution.py:75
  134.7 3.3 %fusion.54 = (bf16[6144,128]{0,1:T(8,128)(2,1)S(1)}, bf16[6144,128]{0,1:T(8,128)(2,1)}) fusion(bf16[6144,256]{0,1:T(8,128)(2,1)} %all-gather.2.cloned.1.call-done), kind=kLoop, calls=%fused_computation.129 | loop fusion | bytes 6291456 | tf_op jit(solution)/shard_map/split | solution.py:76
  137.9 51.5 %while.40 = (s32[]{:T(128)}, f32[1,384]{1,0:T(1,128)S(1)}, f32[1,384]{1,0:T(1,128)S(1)}, f32[384,1,128]{0,2,1:T(8,128)S(1)}, s32[16]{0:T(128)S(1)}, /*index=5*/s...) while((s32[]{:T(128)}, f32[1,384]{1,0:T(1,128)S(1)}, ...), condition=%wide.region_15.16_spmd.clone, body=%wide.region_12.15_spmd.clone.sunk | while | flops 77416712 | bytes 2498271 | solution.py:231
  139.4 1.2 fusion.86
  149.1 1.2 fusion.86
  152.3 1.2 fusion.86
  158.7 1.2 fusion.86
  162.0 1.2 fusion.86
  165.2 1.2 fusion.86
  174.8 1.2 fusion.86
  184.5 1.2 fusion.86
  187.7 1.2 fusion.86
  190.1 32.9 %all_to_all.21 = bf16[32,12,1024]{2,1,0:T(8,128)(2,1)S(1)} all-to-all(bf16[32,12,1024]{2,1,0:T(8,128)(2,1)S(1)} %reshape.275), channel_id=1, replica_groups=mesh['bytes'=16,'ctx'=8,'tp'=4] {'ctx','tp'}, dimensions={0} | all-to-all | bytes 1572864 | tf_op jit(solution)/shard_map/all_to_all | solution.py:86
  224.3 4.6 %all-to-all-start.3 = ((bf16[32,12,1024]{2,1,0:T(8,128)(2,1)}), bf16[32,12,1024]{2,1,0:T(8,128)(2,1)S(1)}, u32[]{:S(2)}, u32[]{:S(2)}) async-start(bf16[32,12,1024]{2,1,0:T(8,128)(2,1)} %broadcast_in_dim.123), calls=%async_computation.3 | async-start | bytes 2097152 | tf_op jit(solution)/shard_map/all_to_all | solution.py:58
  230.4 14.9 %all-to-all-done.3 = bf16[32,12,1024]{2,1,0:T(8,128)(2,1)S(1)} async-done(((bf16[32,12,1024]{2,1,0:T(8,128)(2,1)}), bf16[32,12,1024]{2,1,0:T(8,128)(2,1)S(1)}, u32[]{:S(2)}, u32[]{:S(2)}) %all-to-all-start.3) | async-done | bytes 786464 | tf_op jit(solution)/shard_map/all_to_all | solution.py:58
  (303 shorter events, 51.9 us)
Async XLA Ops:
  6.5 15.3 %copy-start = (bf16[256,1024]{1,0:T(8,128)(2,1)S(1)}, bf16[256,1024]{1,0:T(8,128)(2,1)}, u32[]{:S(2)}) copy-start(bf16[256,1024]{1,0:T(8,128)(2,1)} %param.16) | copy-start | bytes 1572868
  6.5 23.6 %collective-permute-start = (s32[192]{0:T(256)}, s32[192]{0:T(256)S(1)}, u32[]{:S(2)}, u32[]{:S(2)}) collective-permute-start(s32[192]{0:T(256)} %param.14), channel_id=1, source_target_pairs={{0,4},{4,8},{8,12},{12,16},{16,20},{20,24},{24,28},{28,32},{32,36}... | collective-permute-start | bytes 2312 | tf_op jit(solution)/shard_map/ppermute | solution.py:53
  14.3 14.2 %all-to-all-start = ((s32[32,1,1]{2,1,0:T(1,128)}), s32[32,1,1]{2,1,0:T(1,128)S(1)}, u32[]{:S(2)}, u32[]{:S(2)}) async-start(s32[32,1,1]{2,1,0:T(1,128)} %broadcast_in_dim.114), calls=%async_computation | async-start | bytes 32768 | tf_op jit(solution)/shard_map/all_to_all | solution.py:58
  21.8 1.3 copy-start.1
  23.0 1.0 copy-start.3
  23.1 1.2 copy-start.2
  34.5 24.2 %all-to-all-start.1 = ((bf16[32,72,256]{2,1,0:T(8,128)(2,1)}), bf16[32,72,256]{2,1,0:T(8,128)(2,1)S(1)}, u32[]{:S(2)}, u32[]{:S(2)}) async-start(bf16[32,72,256]{2,1,0:T(8,128)(2,1)} %broadcast_in_dim.122), calls=%async_computation.1 | async-start | bytes 2359296 | tf_op jit(solution)/shard_map/all_to_all | solution.py:58
  38.8 95.9 %all-gather.2.cloned.1.call-start = ((), (), s32[]{:S(2)}) async-start(), calls=%async_computation.4 | async-start | bytes 3342336 | tf_op jit(solution)/shard_map/all_gather | solution.py:75
  59.4 2.3 copy-start.5
  61.5 1.0 copy-start.6
  64.3 60.7 %copy-start.7 = (bf16[1024,128]{1,0:T(8,128)(2,1)S(1)}, bf16[1024,128]{1,0:T(8,128)(2,1)}, u32[]{:S(2)}) copy-start(bf16[1024,128]{1,0:T(8,128)(2,1)} %param.20) | copy-start | bytes 786436
  66.9 12.7 %collective-permute-start.1 = (s32[384]{0:T(512)S(1)}, s32[384]{0:T(512)S(1)}, u32[]{:S(2)}, u32[]{:S(2)}) collective-permute-start(s32[384]{0:T(512)S(1)} %fusion.42), channel_id=1, source_target_pairs={{0,32},{32,64},{64,96},{96,128},{128,160},{160,192},{192,224},{224... | collective-permute-start | bytes 4616 | tf_op jit(solution)/shard_map/ppermute | solution.py:35
  70.4 11.1 %collective-permute-start.9 = (s32[384]{0:T(512)S(1)}, s32[384]{0:T(512)S(1)}, u32[]{:S(2)}, u32[]{:S(2)}) collective-permute-start(s32[384]{0:T(512)S(1)} %fusion.42), channel_id=1, source_target_pairs={{32,0},{64,32},{96,64},{128,96},{160,128},{192,160},{224,192},{256... | collective-permute-start | bytes 4616 | tf_op jit(solution)/shard_map/ppermute | solution.py:38
  79.6 6.5 %collective-permute-start.2 = (s32[384]{0:T(512)S(1)}, s32[384]{0:T(512)S(1)}, u32[]{:S(2)}, u32[]{:S(2)}) collective-permute-start(s32[384]{0:T(512)S(1)} %collective-permute-done.1), channel_id=1, source_target_pairs={{0,32},{32,64},{64,96},{96,128},{128,160},{160,192},{192,224},{224... | collective-permute-start | bytes 4616 | tf_op jit(solution)/shard_map/ppermute | solution.py:35
  81.5 6.5 %collective-permute-start.10 = (s32[384]{0:T(512)S(1)}, s32[384]{0:T(512)S(1)}, u32[]{:S(2)}, u32[]{:S(2)}) collective-permute-start(s32[384]{0:T(512)S(1)} %collective-permute-done.9), channel_id=1, source_target_pairs={{32,0},{64,32},{96,64},{128,96},{160,128},{192,160},{224,192},{256... | collective-permute-start | bytes 4616 | tf_op jit(solution)/shard_map/ppermute | solution.py:38
  86.1 6.5 %collective-permute-start.3 = (s32[384]{0:T(512)S(1)}, s32[384]{0:T(512)S(1)}, u32[]{:S(2)}, u32[]{:S(2)}) collective-permute-start(s32[384]{0:T(512)S(1)} %collective-permute-done.2), channel_id=1, source_target_pairs={{0,32},{32,64},{64,96},{96,128},{128,160},{160,192},{192,224},{224... | collective-permute-start | bytes 4616 | tf_op jit(solution)/shard_map/ppermute | solution.py:35
  88.0 6.5 %collective-permute-start.11 = (s32[384]{0:T(512)S(1)}, s32[384]{0:T(512)S(1)}, u32[]{:S(2)}, u32[]{:S(2)}) collective-permute-start(s32[384]{0:T(512)S(1)} %collective-permute-done.10), channel_id=1, source_target_pairs={{32,0},{64,32},{96,64},{128,96},{160,128},{192,160},{224,192},{256... | collective-permute-start | bytes 4616 | tf_op jit(solution)/shard_map/ppermute | solution.py:38
  92.6 6.5 %collective-permute-start.4 = (s32[384]{0:T(512)S(1)}, s32[384]{0:T(512)S(1)}, u32[]{:S(2)}, u32[]{:S(2)}) collective-permute-start(s32[384]{0:T(512)S(1)} %collective-permute-done.3), channel_id=1, source_target_pairs={{0,32},{32,64},{64,96},{96,128},{128,160},{160,192},{192,224},{224... | collective-permute-start | bytes 4616 | tf_op jit(solution)/shard_map/ppermute | solution.py:35
  94.6 6.5 %collective-permute-start.12 = (s32[384]{0:T(512)S(1)}, s32[384]{0:T(512)S(1)}, u32[]{:S(2)}, u32[]{:S(2)}) collective-permute-start(s32[384]{0:T(512)S(1)} %collective-permute-done.11), channel_id=1, source_target_pairs={{32,0},{64,32},{96,64},{128,96},{160,128},{192,160},{224,192},{256... | collective-permute-start | bytes 4616 | tf_op jit(solution)/shard_map/ppermute | solution.py:38
  99.2 6.5 %collective-permute-start.5 = (s32[384]{0:T(512)S(1)}, s32[384]{0:T(512)S(1)}, u32[]{:S(2)}, u32[]{:S(2)}) collective-permute-start(s32[384]{0:T(512)S(1)} %collective-permute-done.4), channel_id=1, source_target_pairs={{0,32},{32,64},{64,96},{96,128},{128,160},{160,192},{192,224},{224... | collective-permute-start | bytes 4616 | tf_op jit(solution)/shard_map/ppermute | solution.py:35
  101.1 6.5 %collective-permute-start.13 = (s32[384]{0:T(512)S(1)}, s32[384]{0:T(512)S(1)}, u32[]{:S(2)}, u32[]{:S(2)}) collective-permute-start(s32[384]{0:T(512)S(1)} %collective-permute-done.12), channel_id=1, source_target_pairs={{32,0},{64,32},{96,64},{128,96},{160,128},{192,160},{224,192},{256... | collective-permute-start | bytes 4616 | tf_op jit(solution)/shard_map/ppermute | solution.py:38
  105.7 6.5 %collective-permute-start.6 = (s32[384]{0:T(512)S(1)}, s32[384]{0:T(512)S(1)}, u32[]{:S(2)}, u32[]{:S(2)}) collective-permute-start(s32[384]{0:T(512)S(1)} %collective-permute-done.5), channel_id=1, source_target_pairs={{0,32},{32,64},{64,96},{96,128},{128,160},{160,192},{192,224},{224... | collective-permute-start | bytes 4616 | tf_op jit(solution)/shard_map/ppermute | solution.py:35
  107.7 6.6 %collective-permute-start.14 = (s32[384]{0:T(512)S(1)}, s32[384]{0:T(512)S(1)}, u32[]{:S(2)}, u32[]{:S(2)}) collective-permute-start(s32[384]{0:T(512)S(1)} %collective-permute-done.13), channel_id=1, source_target_pairs={{32,0},{64,32},{96,64},{128,96},{160,128},{192,160},{224,192},{256... | collective-permute-start | bytes 4616 | tf_op jit(solution)/shard_map/ppermute | solution.py:38
  112.2 6.6 %collective-permute-start.7 = (s32[384]{0:T(512)S(1)}, s32[384]{0:T(512)S(1)}, u32[]{:S(2)}, u32[]{:S(2)}) collective-permute-start(s32[384]{0:T(512)S(1)} %collective-permute-done.6), channel_id=1, source_target_pairs={{0,32},{32,64},{64,96},{96,128},{128,160},{160,192},{192,224},{224... | collective-permute-start | bytes 4616 | tf_op jit(solution)/shard_map/ppermute | solution.py:35
  114.2 7.3 %collective-permute-start.15 = (s32[384]{0:T(512)S(1)}, s32[384]{0:T(512)S(1)}, u32[]{:S(2)}, u32[]{:S(2)}) collective-permute-start(s32[384]{0:T(512)S(1)} %collective-permute-done.14), channel_id=1, source_target_pairs={{32,0},{64,32},{96,64},{128,96},{160,128},{192,160},{224,192},{256... | collective-permute-start | bytes 4616 | tf_op jit(solution)/shard_map/ppermute | solution.py:38
  118.8 5.5 %collective-permute-start.8 = (s32[384]{0:T(512)S(1)}, s32[384]{0:T(512)S(1)}, u32[]{:S(2)}, u32[]{:S(2)}) collective-permute-start(s32[384]{0:T(512)S(1)} %collective-permute-done.7), channel_id=1, source_target_pairs={{0,32},{32,64},{64,96},{96,128},{128,160},{160,192},{192,224},{224... | collective-permute-start | bytes 4616 | tf_op jit(solution)/shard_map/ppermute | solution.py:35
  137.9 51.6 %copy-start.4 = (bf16[128,1024]{1,0:T(8,128)(2,1)S(1)}, bf16[128,1024]{1,0:T(8,128)(2,1)}, u32[]{:S(2)}) copy-start(bf16[128,1024]{1,0:T(8,128)(2,1)} %param.23) | copy-start | bytes 786436
  224.3 21.0 %all-to-all-start.3 = ((bf16[32,12,1024]{2,1,0:T(8,128)(2,1)}), bf16[32,12,1024]{2,1,0:T(8,128)(2,1)S(1)}, u32[]{:S(2)}, u32[]{:S(2)}) async-start(bf16[32,12,1024]{2,1,0:T(8,128)(2,1)} %broadcast_in_dim.123), calls=%async_computation.3 | async-start | bytes 2097152 | tf_op jit(solution)/shard_map/all_to_all | solution.py:58
Sparse Core Ops, SparseCore 0:
  63.8 70.7 all-gather.1
